TPU v7x, 32 devices: a whole 2x2x4 slice. The times are simulated.
32 devices in a mesh: seq: 8 (over z, y), head: 4 (over x, core).
Axes of the slice: x: 2, y: 2, z: 4, core: 2. Of those that a mesh axis runs over, the one named last changes fastest.
Arguments:
- patches: bfloat16 [2048, 1280], P('seq'), may hold values from -6 to 6
- norm_gain: float32 [1280], replicated, may hold values from 0.5 to 1.5
- w_qkv: bfloat16 [1280, 3, 1280], P('seq', None, 'head'), as said below
- w_out: bfloat16 [1280, 1280], P('head', 'seq'), may hold values from -0.15625 to 0.15625
- window_order: int32 [8, 64], P('seq'), may hold values from 0 to 63, each once within a row
- merge_gain: float32 [1280], replicated, may hold values from 0.5 to 1.5
- w_kv: bfloat16 [5120, 2, 1024], P('seq', None, 'head'), as said below
- queries: bfloat16 [16, 8192], P('seq', 'head'), may hold values from -6 to 6
- suffix_kv: bfloat16 [16, 64, 2, 1024], P('seq', None, None, 'head'), may hold values from -12 to 12
- question_lengths: int32 [16], P('seq'), may hold values from 1 to 64
- frame_range: int32 [16, 2], replicated, may hold values from 0 to 8, as said below
Outputs:
- answers: bfloat16 [16, 8192], P('seq', 'head')
Inputs may be any that keep to these rules, and one draw needn't show every extreme that they name: `window_order`: each row is an ordering of a frame's units; positions w * 16 to (w + 1) * 16 - 1 form window w. `frame_range`: the first entry of a row is below the second. `w_qkv`: entries of order one over the square root of 1280. `w_kv`: entries of order one over the square root of 5120.
All inputs are finite; a program needn't handle non-finite values.
Results may differ from a plain program's by a relative error of at most 0.007.
Values may be sent and summed in bfloat16 or wider, within the bound.
A program may use at most 64 MiB of HBM per device.

v0:
```python
import jax
import jax.numpy as jnp
from jax import lax
from jax.sharding import PartitionSpec as P

VD = 1280
VH = 16
HD = 128
FPATCH = 256
WIN = 64


NEGATIVE = -1e30


def rms_scale(values, gain):
    return values * lax.rsqrt(jnp.mean(values * values, axis=-1, keepdims=True) + 1e-06) * gain


def frame_window(frame_rows, unit_order, local_heads, head_size):
    unit_count = unit_order.shape[0]
    grouped = frame_rows.reshape(unit_count, 4, 3, local_heads * head_size)[unit_order]
    windows = grouped.reshape(-1, WIN, 3, local_heads, head_size)
    scores = jnp.einsum(
        "wqhd,wkhd->whqk", windows[:, :, 0], windows[:, :, 1], preferred_element_type=jnp.float32
    ) * head_size ** (-0.5)
    weights = jax.nn.softmax(scores, axis=-1).astype(jnp.bfloat16)
    mixed = jnp.einsum(
        "whqk,wkhd->wqhd", weights, windows[:, :, 2], preferred_element_type=jnp.float32
    ).astype(jnp.bfloat16)
    mixed = mixed.reshape(unit_count, 4, local_heads * head_size)
    return (
        jnp.zeros_like(mixed)
        .at[unit_order]
        .set(mixed)
        .reshape(unit_count * 4, local_heads * head_size)
    )


def prefix_scores(asking, keys_values, bounds, frame_tokens):
    token_count = keys_values.shape[0]
    kv_local, head_size = (asking.shape[1], asking.shape[3])
    keys = keys_values[:, 0].reshape(token_count, kv_local, head_size)
    values = keys_values[:, 1].reshape(token_count, kv_local, head_size)
    frame_index = jnp.arange(token_count) // frame_tokens
    live = (frame_index[None, :] >= bounds[:, 0:1]) & (frame_index[None, :] < bounds[:, 1:2])
    scores = jnp.einsum(
        "qgjd,ngd->qgjn", asking, keys, preferred_element_type=jnp.float32
    ) * head_size ** (-0.5)
    return (jnp.where(live[:, None, None, :], scores, -jnp.inf), values)


def add_suffix(maxima, totals, weighted, asking, suffix_kv, lengths):
    quest_count, span = (suffix_kv.shape[0], suffix_kv.shape[1])
    kv_local, head_size = (asking.shape[1], asking.shape[3])
    keys = suffix_kv[:, :, 0].reshape(quest_count, span, kv_local, head_size)
    values = suffix_kv[:, :, 1].reshape(quest_count, span, kv_local, head_size)
    scores = jnp.einsum(
        "qgjd,qsgd->qgjs", asking, keys, preferred_element_type=jnp.float32
    ) * head_size ** (-0.5)
    live = (jnp.arange(span)[None, :] < lengths[:, None])[:, None, None, :]
    scores = jnp.where(live, scores, -jnp.inf)
    highest = jnp.maximum(maxima, jnp.max(scores, axis=-1))
    weights = jnp.exp(scores - highest[..., None])
    carried = jnp.exp(maxima - highest)
    totals = totals * carried + jnp.sum(weights, axis=-1)
    weighted = weighted * carried[..., None] + jnp.einsum(
        "qgjs,qsgd->qgjd", weights.astype(jnp.bfloat16), values, preferred_element_type=jnp.float32
    )
    return (weighted / totals[..., None]).reshape(quest_count, -1).astype(jnp.bfloat16)


def on_device(
    patches,
    norm_gain,
    w_qkv,
    w_out,
    window_order,
    merge_gain,
    w_kv,
    queries,
    suffix_kv,
    question_lengths,
    frame_range,
):
    head_count = lax.axis_size("head")
    row_count = patches.shape[0]
    columns = w_qkv.shape[2]
    head_size = VD // VH
    local_heads = columns // head_size
    source = patches.astype(jnp.float32)
    normed = rms_scale(source, norm_gain).astype(jnp.bfloat16)
    portion = lax.all_gather(w_qkv, "seq", axis=0, tiled=True)
    inputs = normed
    projected = jnp.dot(
        inputs, portion.reshape(portion.shape[0], 3 * columns), preferred_element_type=jnp.float32
    )
    projected = projected.astype(jnp.bfloat16).reshape(window_order.shape[0], -1, 3, columns)
    attended = jax.vmap(
        lambda frame_rows, unit_order: frame_window(frame_rows, unit_order, local_heads, head_size)
    )(projected, window_order)
    attended = attended.reshape(row_count, columns)
    w_full = lax.all_gather(w_out, "seq", axis=1, tiled=True)
    share_rows = row_count // head_count
    shared = lax.psum_scatter(
        jnp.dot(attended, w_full, preferred_element_type=jnp.float32).astype(jnp.bfloat16),
        "head",
        scatter_dimension=0,
        tiled=True,
    ).astype(jnp.float32)
    own_rows = lax.dynamic_slice_in_dim(source, lax.axis_index("head") * share_rows, share_rows, 0)
    merged = (
        rms_scale(own_rows + shared, merge_gain)
        .astype(jnp.bfloat16)
        .reshape(share_rows // 4, 4 * VD)
    )
    merged_all = lax.all_gather(merged, "head", axis=0, tiled=True)
    token_count = merged_all.shape[0]
    kv_columns = w_kv.shape[2]
    portion = lax.all_gather(w_kv, "seq", axis=0, tiled=True)
    inputs = merged_all
    visual = jnp.dot(
        inputs,
        portion.reshape(portion.shape[0], 2 * kv_columns),
        preferred_element_type=jnp.float32,
    )
    visual = visual.astype(jnp.bfloat16).reshape(token_count, 2, kv_columns)
    quest_count = queries.shape[0]
    kv_local = kv_columns // HD
    asking = queries.reshape(quest_count, kv_local, -1, HD)
    group = asking.shape[2]
    frame_tokens = FPATCH // 4
    seq_index = lax.axis_index("seq")
    own_bounds = lax.dynamic_slice_in_dim(frame_range, seq_index * quest_count, quest_count, 0)
    maxima = jnp.full((quest_count, kv_local, group), NEGATIVE, jnp.float32)
    scores, values = prefix_scores(
        asking, lax.all_gather(visual, "seq", axis=0, tiled=True), own_bounds, frame_tokens
    )
    highest = jnp.maximum(maxima, jnp.max(scores, axis=-1))
    weights = jnp.exp(scores - highest[..., None])
    totals = jnp.sum(weights, axis=-1)
    weighted = jnp.einsum(
        "qgjn,ngd->qgjd", weights.astype(jnp.bfloat16), values, preferred_element_type=jnp.float32
    )
    maxima, totals, weighted = (highest, totals, weighted)
    return add_suffix(maxima, totals, weighted, asking, suffix_kv, question_lengths)


def solution(mesh):
    placed = (
        P("seq", None),
        P(),
        P("seq", None, "head"),
        P("head", "seq"),
        P("seq", None),
        P(),
        P("seq", None, "head"),
        P("seq", "head"),
        P("seq", None, None, "head"),
        P("seq"),
        P(),
    )
    return jax.shard_map(
        on_device, mesh=mesh, in_specs=placed, out_specs=P("seq", "head"), check_vma=False
    )
```

profile of v0, /device:TPU:0, one launch (start us, length us, event | category | flops | bytes accessed | tf_op | source)
XLA Modules:
  0.0 248.2 jit_solution(14426382259012664748)
XLA Ops:
  6.5 0.7 all-gather.3.cloned.1.call-update
  7.3 0.7 fusion.30
  8.0 1.3 multiply_reduce_fusion
  9.3 37.0 %all_gather.16 = bf16[320,1280]{0,1:T(8,128)(2,1)S(1)} all-gather(bf16[320,160]{0,1:T(8,128)(2,1)} %param.14), channel_id=1, replica_groups=mesh['seq'=8,'head'=4] {'seq'}, dimensions={1}, use_global_device_ids=true | all-gather | bytes 921600 | tf_op jit(solution)/shard_map/all_gather | solution.py:103
  46.3 29.9 %all-gather.3.cloned.1.call-done = bf16[1280,3,320]{2,0,1:T(8,128)(2,1)} async-done(((bf16[160,3,320]{2,0,1:T(8,128)(2,1)}), bf16[1280,3,320]{2,0,1:T(8,128)(2,1)}) %all-gather.3.cloned.1.call-update) | async-done | bytes 2457616 | tf_op jit(solution)/shard_map/all_gather | solution.py:93
  76.2 5.3 %copy.55 = bf16[1280,3,320]{0,2,1:T(8,128)(2,1)} copy(bf16[1280,3,320]{2,0,1:T(8,128)(2,1)} %all-gather.3.cloned.1.call-done) | data formatting | bytes 4915200 | tf_op jit(solution)/shard_map/all_gather | solution.py:93
  81.5 2.6 %convolution_convert_fusion.1 = bf16[256,960]{0,1:T(8,128)(2,1)S(1)} fusion(bf16[1280,960]{0,1:T(8,128)(2,1)} %bitcast.98, f32[1280]{0:T(1024)S(1)} %copy-done.5, f32[256]{0:T(256)S(1)} %add_rsqrt_fusion, bf16[256,1280]{1,0:T(8,128)(2,1)S(1)} %copy-done.1), kind=kOutput, calls=%fused_computation.7 | convolution fusion | flops 630702080 | bytes 3610624 | tf_op jit(solution)/shard_map/dot_general | solution.py:95
  85.0 1.1 gather_fusion
  86.4 0.6 reshape.180
  88.7 2.5 scatter_fusion
  91.3 1.4 convolution_convert_fusion
  92.8 0.7 all-gather.5.cloned.1.call-update
  94.6 19.3 %reduce-scatter.2.cloned.1.call-done = bf16[64,1280]{1,0:T(8,128)(2,1)} async-done(((bf16[256,1280]{1,0:T(8,128)(2,1)}), bf16[64,1280]{1,0:T(8,128)(2,1)}) %reduce-scatter.2.cloned.1.call-update) | async-done | bytes 163856 | tf_op jit(solution)/shard_map/reduce_scatter | solution.py:105
  113.9 1.1 multiply_reduce_fusion.1
  115.0 1.0 multiply_convert_fusion.2
  116.2 7.3 %all_gather.17 = bf16[64,5120]{1,0:T(8,128)(2,1)S(1)} all-gather(bf16[16,5120]{1,0:T(8,128)(2,1)S(1)} %reshape.186), channel_id=1, replica_groups=mesh['seq'=8,'head'=4] {'head'}, dimensions={0}, use_global_device_ids=true | all-gather | bytes 819200 | tf_op jit(solution)/shard_map/all_gather | solution.py:117
  123.5 78.6 %all-gather.5.cloned.1.call-done = bf16[5120,2,256]{2,1,0:T(2,128)(2,1)} async-done(((bf16[640,2,256]{2,1,0:T(2,128)(2,1)}), bf16[5120,2,256]{2,1,0:T(2,128)(2,1)}) %all-gather.5.cloned.1.call-update) | async-done | bytes 5242896 | tf_op jit(solution)/shard_map/all_gather | solution.py:120
  202.1 3.4 %copy.94 = bf16[640,8,2,256]{3,1,2,0:T(8,128)(2,1)S(1)} copy(bf16[640,8,2,256]{3,2,1,0:T(2,128)(2,1)} %bitcast.97) | data formatting | bytes 10485760
  205.4 1.0 convolution_convert_fusion.3
  206.5 31.5 %all_gather.19 = bf16[512,2,256]{2,1,0:T(2,128)(2,1)S(1)} all-gather(bf16[64,2,256]{2,1,0:T(2,128)(2,1)S(1)} %reshape.188), channel_id=1, replica_groups=mesh['seq'=8,'head'=4] {'seq'}, dimensions={0}, use_global_device_ids=true | all-gather | bytes 589824 | tf_op jit(solution)/shard_map/all_gather | solution.py:137
  238.0 0.7 fusion.34
  238.7 0.7 copy.91
  239.6 0.7 copy.90
  241.0 0.6 copy.140
  (53 shorter events, 5.3 us)
Async XLA Ops:
  6.5 87.1 %copy-start = (s32[16,2]{0,1:T(2,128)S(1)}, s32[16,2]{0,1:T(2,128)}, u32[]{:S(2)}) copy-start(s32[16,2]{0,1:T(2,128)} %param.21) | copy-start | bytes 388
  6.5 69.7 %all-gather.3.cloned.1.call-start = ((), (), s32[]{:S(2)}) async-start(), calls=%async_computation.1 | async-start | bytes 3317760 | tf_op jit(solution)/shard_map/all_gather | solution.py:93
  7.3 106.7 %reduce-scatter.2.cloned.1.call-start = ((), (), s32[]{:S(2)}) async-start(), calls=%async_computation.2 | async-start | bytes 819200 | tf_op jit(solution)/shard_map/reduce_scatter | solution.py:105
  46.3 35.2 %copy-start.1 = (bf16[256,1280]{1,0:T(8,128)(2,1)S(1)}, bf16[256,1280]{1,0:T(8,128)(2,1)}, u32[]{:S(2)}) copy-start(bf16[256,1280]{1,0:T(8,128)(2,1)} %param.11) | copy-start | bytes 1966084
  46.3 35.2 %copy-start.5 = (f32[1280]{0:T(1024)S(1)}, f32[1280]{0:T(1024)}, u32[]{:S(2)}) copy-start(f32[1280]{0:T(1024)} %param.12) | copy-start | bytes 15364
  92.7 1.0 copy-start.2
  92.7 109.3 %all-gather.5.cloned.1.call-start = ((), (), s32[]{:S(2)}) async-start(), calls=%async_computation.3 | async-start | bytes 5898240 | tf_op jit(solution)/shard_map/all_gather | solution.py:120
  93.5 0.8 copy-start.6
  93.5 0.9 copy-start.3
  93.5 21.5 %copy-start.4 = (f32[1280]{0:T(1024)S(1)}, f32[1280]{0:T(1024)}, u32[]{:S(2)}) copy-start(f32[1280]{0:T(1024)} %param.16) | copy-start | bytes 15364
Sparse Core Ops, SparseCore 0:
  9.5 66.6 all-gather.2
  92.8 21.0 reduce-scatter.1
  116.1 85.8 all-gather.4
where the time goes:
time: 249 us; the launch traced here: 248 us
  waiting for transfers between devices  129 us (52%)
  blocking collectives  75.8 us (30%)
  local copies, waits for them, and re-layouts  18.3 us (7%)
  between operations  13.4 us (5%)
  matrix products  6.75 us (3%)
  other arithmetic  4.65 us (2%)
    all_gather x1, waiting for transfers between devices, on_device(): portion = lax.all_gather(w_kv, 'seq', axis=0, tiled=True)  78.6 us
    all_gather x1, blocking collectives, on_device(): w_full = lax.all_gather(w_out, 'seq', axis=1, tiled=True)  37 us
    all_gather x1, blocking collectives, on_device(): lax.all_gather(visual, 'seq', axis=0, tiled=True)  31.5 us
    all_gather x1, waiting for transfers between devices, on_device(): portion = lax.all_gather(w_qkv, 'seq', axis=0, tiled=True)  29.9 us
    reduce_scatter x1, waiting for transfers between devices, on_device(): lax.psum_scatter(jnp.dot(attended, w_full, preferred_element_type=jnp.flo...  19.3 us
    all_gather x1, blocking collectives, on_device(): merged_all = lax.all_gather(merged, 'head', axis=0, tiled=True)  7.31 us
    unnamed x18, local copies, waits for them, and re-layouts  5.36 us
    all_gather x1, local copies, waits for them, and re-layouts, on_device(): portion = lax.all_gather(w_qkv, 'seq', axis=0, tiled=True)  5.29 us
  transfers between devices with their start and end apart: 3, of which 3 were waited for; matrix products, arithmetic and copies ran while one was open for 2% of the time, Pallas kernels for 0%

commit v1 on v0

v1 whole, which is shorter than its diff:
```python
import functools

import jax
import jax.numpy as jnp
from jax import lax
from jax.experimental import pallas as pl
from jax.experimental.pallas import tpu as pltpu
from jax.sharding import PartitionSpec as P

VD = 1280
VH = 16
HD = 128
FPATCH = 256
WIN = 64

MESH = pl.DeviceIdType.MESH
VMEM = pl.BlockSpec(memory_space=pltpu.VMEM)


def rms_scale(values, gain):
    return values * lax.rsqrt(jnp.mean(values * values, axis=-1, keepdims=True) + 1e-06) * gain


def exchange_kernel(axis, count, gather, x_ref, out_ref, send_sem, recv_sem, own_sem):
    me = lax.axis_index(axis)
    barrier = pltpu.get_barrier_semaphore()
    for step in range(1, count):
        pl.semaphore_signal(
            barrier, inc=1, device_id={axis: lax.rem(me + step, count)}, device_id_type=MESH
        )
    pl.semaphore_wait(barrier, count - 1)
    copies = []
    for step in range(1, count):
        peer = lax.rem(me + step, count)
        copy = pltpu.make_async_remote_copy(
            src_ref=x_ref if gather else x_ref.at[peer],
            dst_ref=out_ref.at[me],
            send_sem=send_sem.at[step],
            recv_sem=recv_sem.at[step],
            device_id={axis: peer},
            device_id_type=MESH,
        )
        copy.start()
        copies.append(copy)
    own = pltpu.make_async_copy(x_ref if gather else x_ref.at[me], out_ref.at[me], own_sem)
    own.start()
    own.wait()
    for copy in copies:
        copy.wait()


def exchange(x, axis, gather, collective_id):
    count = lax.axis_size(axis)
    shape = ((count,) + x.shape) if gather else x.shape
    return pl.pallas_call(
        functools.partial(exchange_kernel, axis, count, gather),
        out_shape=jax.ShapeDtypeStruct(shape, x.dtype),
        in_specs=[VMEM],
        out_specs=VMEM,
        scratch_shapes=[
            pltpu.SemaphoreType.DMA((count,)),
            pltpu.SemaphoreType.DMA((count,)),
            pltpu.SemaphoreType.DMA,
        ],
        compiler_params=pltpu.CompilerParams(collective_id=collective_id, has_side_effects=True),
        name=f"exchange_{collective_id}",
    )(x)


def ring_kernel(count, qkv_ref, wout_ref, qkv_out, wout_out, send_sem, recv_sem, own_sem):
    me = lax.axis_index("seq")
    odd = lax.rem(me, 2)
    place = (1 - odd) * (me // 2) + odd * (count - 1 - me // 2)

    def index_of(position):
        position = lax.rem(position + count, count)
        late = position // (count // 2)
        return (1 - late) * 2 * position + late * (2 * (count - 1 - position) + 1)

    neighbours = (index_of(place + 1), index_of(place - 1))
    barrier = pltpu.get_barrier_semaphore()
    for neighbour in neighbours:
        pl.semaphore_signal(barrier, inc=1, device_id={"seq": neighbour}, device_id_type=MESH)
    pl.semaphore_wait(barrier, 2)
    far, near = count // 2, count - 1 - count // 2
    pieces = 4

    def slot(piece, source):
        return qkv_out.at[piece, source] if piece < 3 else wout_out.at[source]

    def own(piece):
        return qkv_ref.at[piece] if piece < 3 else wout_ref

    copies = {}
    for step in range(far):
        for piece in range(pieces):
            for way in range(2):
                hops = far if (piece < 2) == (way == 0) else near
                if step >= hops:
                    continue
                source = index_of(place - step if way == 0 else place + step)
                if step > 0:
                    copies[step - 1, piece, way].wait_recv()
                copy = pltpu.make_async_remote_copy(
                    src_ref=own(piece) if step == 0 else slot(piece, source),
                    dst_ref=slot(piece, source),
                    send_sem=send_sem.at[step, piece, way],
                    recv_sem=recv_sem.at[step, piece, way],
                    device_id={"seq": neighbours[way]},
                    device_id_type=MESH,
                )
                copy.start()
                copies[step, piece, way] = copy
    kept = [pltpu.make_async_copy(own(p), slot(p, me), own_sem.at[p]) for p in range(pieces)]
    for copy in kept:
        copy.start()
    for copy in kept:
        copy.wait()
    for (step, piece, way), copy in copies.items():
        if (step + 1, piece, way) not in copies:
            copy.wait_recv()
    for copy in copies.values():
        copy.wait_send()


def ring_weights(w_qkv, w_out):
    count = lax.axis_size("seq")
    far = count // 2
    return pl.pallas_call(
        functools.partial(ring_kernel, count),
        out_shape=(
            jax.ShapeDtypeStruct((3, count) + w_qkv.shape[1:], w_qkv.dtype),
            jax.ShapeDtypeStruct((count,) + w_out.shape, w_out.dtype),
        ),
        in_specs=[VMEM, VMEM],
        out_specs=(VMEM, VMEM),
        scratch_shapes=[
            pltpu.SemaphoreType.DMA((far, 4, 2)),
            pltpu.SemaphoreType.DMA((far, 4, 2)),
            pltpu.SemaphoreType.DMA((4,)),
        ],
        compiler_params=pltpu.CompilerParams(collective_id=0, has_side_effects=True),
        name="ring_weights",
    )(w_qkv, w_out)


def frame_attention(query, key, value, unit_order, head_size):
    unit_count = unit_order.shape[0]
    patch_count = unit_count * 4
    ranks = jnp.sum(
        jnp.where(
            unit_order[None, :] == (jnp.arange(patch_count) // 4)[:, None],
            jnp.arange(unit_count)[None, :] // (WIN // 4),
            0,
        ),
        axis=1,
    )
    same = ranks[:, None] == ranks[None, :]
    scores = jnp.einsum(
        "qhd,khd->hqk", query, key, preferred_element_type=jnp.float32
    ) * head_size ** (-0.5)
    scores = jnp.where(same[None], scores, -jnp.inf)
    weights = jax.nn.softmax(scores, axis=-1).astype(jnp.bfloat16)
    return jnp.einsum(
        "hqk,khd->qhd", weights, value, preferred_element_type=jnp.float32
    ).astype(jnp.bfloat16)


def on_device(
    patches,
    norm_gain,
    w_qkv,
    w_out,
    window_order,
    merge_gain,
    w_kv,
    queries,
    suffix_kv,
    question_lengths,
    frame_range,
):
    head_count = lax.axis_size("head")
    seq_count = lax.axis_size("seq")
    row_count = patches.shape[0]
    frame_count = window_order.shape[0]
    columns = w_qkv.shape[2]
    head_size = VD // VH
    local_heads = columns // head_size
    source = patches.astype(jnp.float32)
    normed = rms_scale(source, norm_gain).astype(jnp.bfloat16)
    qkv_all, w_out_all = ring_weights(w_qkv.transpose(1, 0, 2), w_out)
    qkv_all = qkv_all.reshape(3, -1, columns)
    query, key, value = [
        jnp.dot(normed, qkv_all[part], preferred_element_type=jnp.float32)
        .astype(jnp.bfloat16)
        .reshape(frame_count, -1, local_heads, head_size)
        for part in range(3)
    ]
    attended = jax.vmap(
        lambda q, k, v, order: frame_attention(q, k, v, order, head_size)
    )(query, key, value, window_order).reshape(row_count, columns)
    w_full = w_out_all.transpose(1, 0, 2).reshape(columns, VD)
    share_rows = row_count // head_count
    partial = jnp.dot(attended, w_full, preferred_element_type=jnp.float32).astype(jnp.bfloat16)
    parts = exchange(partial.reshape(head_count, share_rows, VD), "head", False, 1)
    shared = jnp.sum(parts.astype(jnp.float32), axis=0)
    own_rows = lax.dynamic_slice_in_dim(source, lax.axis_index("head") * share_rows, share_rows, 0)
    merged = rms_scale(own_rows + shared, merge_gain).astype(jnp.bfloat16)
    share_tokens = share_rows // 4
    depth = w_kv.shape[0]
    merged = merged.reshape(share_tokens, seq_count, depth).transpose(1, 0, 2)
    merged = exchange(merged, "seq", False, 2)
    merged = exchange(merged, "head", True, 3)
    merged = merged.transpose(1, 0, 2, 3).reshape(-1, depth)
    kv_columns = w_kv.shape[2]
    partial = jnp.dot(
        merged, w_kv.reshape(depth, 2 * kv_columns), preferred_element_type=jnp.float32
    )
    parts = exchange(partial.reshape(seq_count, -1, 2 * kv_columns), "seq", False, 4)
    visual = jnp.sum(parts, axis=0).astype(jnp.bfloat16)
    visual = exchange(visual, "seq", True, 5).reshape(-1, 2 * kv_columns)

    token_count = visual.shape[0]
    quest_count = queries.shape[0]
    span = suffix_kv.shape[1]
    kv_local = kv_columns // HD
    asking = queries.reshape(quest_count, kv_local, -1, HD)
    frame_tokens = FPATCH // 4
    seq_index = lax.axis_index("seq")
    bounds = lax.dynamic_slice_in_dim(frame_range, seq_index * quest_count, quest_count, 0)
    frame_index = jnp.arange(token_count) // frame_tokens
    live = (frame_index[None, :] >= bounds[:, 0:1]) & (frame_index[None, :] < bounds[:, 1:2])
    suffix_live = jnp.arange(span)[None, :] < question_lengths[:, None]
    suffix = suffix_kv.reshape(quest_count, span, 2, kv_local, HD)
    answers = []
    for g in range(kv_local):
        ask = asking[:, g]
        keys = visual[:, g * HD : (g + 1) * HD]
        values = visual[:, kv_columns + g * HD : kv_columns + (g + 1) * HD]
        scores = jnp.einsum(
            "qjd,nd->qjn", ask, keys, preferred_element_type=jnp.float32
        ) * HD ** (-0.5)
        scores = jnp.where(live[:, None, :], scores, -jnp.inf)
        tail = jnp.einsum(
            "qjd,qsd->qjs", ask, suffix[:, :, 0, g], preferred_element_type=jnp.float32
        ) * HD ** (-0.5)
        tail = jnp.where(suffix_live[:, None, :], tail, -jnp.inf)
        highest = jnp.maximum(
            jnp.max(scores, axis=-1, keepdims=True), jnp.max(tail, axis=-1, keepdims=True)
        )
        weights = jnp.exp(scores - highest)
        tail_weights = jnp.exp(tail - highest)
        totals = jnp.sum(weights, axis=-1, keepdims=True) + jnp.sum(
            tail_weights, axis=-1, keepdims=True
        )
        mixed = jnp.einsum(
            "qjn,nd->qjd", weights.astype(jnp.bfloat16), values, preferred_element_type=jnp.float32
        ) + jnp.einsum(
            "qjs,qsd->qjd",
            tail_weights.astype(jnp.bfloat16),
            suffix[:, :, 1, g],
            preferred_element_type=jnp.float32,
        )
        answers.append((mixed / totals).astype(jnp.bfloat16))
    return jnp.stack(answers, axis=1).reshape(quest_count, -1)


def solution(mesh):
    placed = (
        P("seq", None),
        P(),
        P("seq", None, "head"),
        P("head", "seq"),
        P("seq", None),
        P(),
        P("seq", None, "head"),
        P("seq", "head"),
        P("seq", None, None, "head"),
        P("seq"),
        P(),
    )
    return jax.shard_map(
        on_device, mesh=mesh, in_specs=placed, out_specs=P("seq", "head"), check_vma=False
    )
```

time: 249 us -> 150 us (0.60)
  waiting for transfers between devices: 129 us -> 0 us
  Pallas kernels: 0 us -> 124 us
  blocking collectives: 75.8 us -> 0 us
  between operations: 13.4 us -> 0.3 us
  local copies, waits for them, and re-layouts: 18.3 us -> 9.33 us
  matrix products: 6.75 us -> 9.54 us
    pallas_call x0 -> x6, Pallas kernels: none -> 124 us  [the longest x5 75.1 us: exchange(): pl.pallas_call(functools.partial(exchange_kernel, axis, count, gather), o...]
    all_gather x2 -> x0, waiting for transfers between devices: 109 us -> none  [the longest x1 78.6 us: on_device(): portion = lax.all_gather(w_kv, 'seq', axis=0, tiled=True)]
    all_gather x3 -> x0, blocking collectives: 75.8 us -> none  [the longest x1 37 us: on_device(): w_full = lax.all_gather(w_out, 'seq', axis=1, tiled=True)]
    reduce_scatter x1 -> x0, waiting for transfers between devices: 19.3 us -> none  [on_device(): lax.psum_scatter(jnp.dot(attended, w_full, preferred_element_type=jnp.flo...]
    all_gather x1 -> x0, local copies, waits for them, and re-layouts: 5.29 us -> none  [on_device(): portion = lax.all_gather(w_qkv, 'seq', axis=0, tiled=True)]
    reduce_sum x1 -> x7, other arithmetic: 0.17 us -> 3.96 us  [the longest x1 1.98 us: on_device(): visual = jnp.sum(parts, axis=0).astype(jnp.bfloat16)]
    dot_general x8 -> x14, matrix products: 5.02 us -> 7.61 us  [the longest x3 1.8 us: on_device(): jnp.dot(normed, qkv_all[part], preferred_element_type=jnp.float32)]
    unnamed x18 -> x25, local copies, waits for them, and re-layouts: 5.36 us -> 3.73 us
  transfers between devices with their start and end apart: 3 -> 0, of which waited for: 3 -> 0; matrix products, arithmetic and copies ran while one was open for 2% -> 0% of each run, Pallas kernels for 0% -> 0%
where the time goes in v1:
time: 150 us; the launch traced here: 148 us
  Pallas kernels  124 us (83%)
  matrix products  9.54 us (6%)
  local copies, waits for them, and re-layouts  9.33 us (6%)
  other arithmetic  4.82 us (3%)
    pallas_call x5, Pallas kernels, exchange(): pl.pallas_call(functools.partial(exchange_kernel, axis, count, gather), o...  75.1 us
    pallas_call x1, Pallas kernels, ring_weights(): pl.pallas_call(functools.partial(ring_kernel, count), out_shape=(jax.Shap...  49 us
    unnamed x25, local copies, waits for them, and re-layouts  3.73 us

profile of v1, /device:TPU:0, one launch (start us, length us, event | category | flops | bytes accessed | tf_op | source)
XLA Modules:
  0.0 148.2 jit_solution(17220411967046519224)
XLA Ops:
  0.0 1.7 %copy.27.wout_ref = bf16[320,160]{1,0:T(8,128)(2,1)} copy(bf16[320,160]{0,1:T(8,128)(2,1)} %param.14) | data formatting | bytes 204800 | tf_op args[3]
  1.7 49.0 %ring_weights.1 = (bf16[3,8,160,320]{3,2,1,0:T(8,128)(2,1)}, bf16[8,320,160]{2,1,0:T(8,128)(2,1)}) custom-call(bf16[3,160,320]{2,1,0:T(8,128)(2,1)} %bitcast.127, bf16[320,160]{1,0:T(8,128)(2,1)} %copy.27.wout_ref), custom_call_target="tpu_custom_call" | custom-call | tf_op jit(solution)/shard_map/ring_weights/pallas_call | solution.py:129
  50.8 2.2 %fusion.40 = (bf16[1,8,160,320]{3,2,1,0:T(8,128)(2,1)S(1)}, bf16[1,8,160,320]{3,2,1,0:T(8,128)(2,1)S(1)}, bf16[1,8,160,320]{3,2,1,0:T(8,128)(2,1)S(1)}) fusion(bf16[3,8,160,320]{3,2,1,0:T(8,128)(2,1)} %get-tuple-element.7), kind=kLoop, calls=%fused_computation.95 | loop fusion | bytes 4915200 | tf_op jit(solution)/shard_map/slice | solution.py:194
  53.2 0.6 convolution_convert_fusion.3
  53.8 0.6 convolution_convert_fusion.2
  55.0 0.5 fusion.42
  55.5 0.6 convolution_convert_fusion.4
  56.5 0.9 copy-done.2
  57.5 0.8 copy.29
  58.2 1.4 convolution_convert_fusion
  59.6 11.0 %exchange_1.1 = bf16[4,64,1280]{2,1,0:T(8,128)(2,1)} custom-call(bf16[4,64,1280]{2,1,0:T(8,128)(2,1)} %bitcast.115), custom_call_target="tpu_custom_call" | custom-call | tf_op jit(solution)/shard_map/exchange_1/pallas_call | solution.py:55
  70.7 1.2 convert_reduce_fusion
  72.2 0.4 copy-done.6
  72.8 0.7 copy.70
  73.4 9.5 %exchange_2.1.x_ref = bf16[8,16,640]{2,1,0:T(8,128)(2,1)} custom-call(bf16[8,16,640]{2,1,0:T(8,128)(2,1)} %bitcast.126), custom_call_target="tpu_custom_call" | custom-call | tf_op jit(solution)/shard_map/exchange_2/pallas_call | solution.py:55
  82.9 9.8 %exchange_3.1 = bf16[4,8,16,640]{3,2,1,0:T(8,128)(2,1)} custom-call(bf16[8,16,640]{2,1,0:T(8,128)(2,1)} %exchange_2.1.x_ref), custom_call_target="tpu_custom_call" | custom-call | tf_op jit(solution)/shard_map/exchange_3/pallas_call | solution.py:55
  92.7 1.2 copy.31
  94.3 1.6 %fusion.47.x_ref = f32[8,64,512]{2,1,0:T(8,128)} fusion(bf16[8,64,640]{2,1,0:T(8,128)(2,1)S(1)} %bitcast.116, bf16[640,512,1]{1,0,2:T(8,128)(2,1)S(1)} %reshape.367), kind=kOutput, calls=%fused_computation.102 | convolution fusion | flops 335544320 | bytes 2359296 | tf_op jit(solution)/shard_map/dot_general | solution.py:216
  95.9 23.9 %exchange_4.1 = f32[8,64,512]{2,1,0:T(8,128)} custom-call(f32[8,64,512]{2,1,0:T(8,128)} %fusion.47.x_ref), custom_call_target="tpu_custom_call" | custom-call | tf_op jit(solution)/shard_map/exchange_4/pallas_call | solution.py:55
  119.8 2.0 %reduce_sum.95.x_ref = bf16[64,512]{1,0:T(8,128)(2,1)} reduce(f32[8,64,512]{2,1,0:T(8,128)} %exchange_4.1, f32[]{:T(128)} %constant.72.clone.1), dimensions={0}, to_apply=%region_6.7 | reduce | flops 229376 | bytes 1114116 | tf_op jit(solution)/shard_map/reduce_sum | solution.py:220
  121.8 21.0 %exchange_5.1 = bf16[8,64,512]{2,1,0:T(8,128)(2,1)} custom-call(bf16[64,512]{1,0:T(8,128)(2,1)} %reduce_sum.95.x_ref), custom_call_target="tpu_custom_call" | custom-call | tf_op jit(solution)/shard_map/exchange_5/pallas_call | solution.py:55
  143.0 1.1 fusion.45
  145.1 1.1 fusion.17
  147.6 0.6 copy.71
  (57 shorter events, 4.5 us)
Async XLA Ops:
  0.0 142.8 %copy-start = (s32[16,2]{0,1:T(2,128)S(1)}, s32[16,2]{0,1:T(2,128)}, u32[]{:S(2)}) copy-start(s32[16,2]{0,1:T(2,128)} %param.21) | copy-start | bytes 388
  50.7 2.2 %copy-start.1 = (bf16[256,1280]{1,0:T(8,128)(2,1)S(1)}, bf16[256,1280]{1,0:T(8,128)(2,1)}, u32[]{:S(2)}) copy-start(bf16[256,1280]{1,0:T(8,128)(2,1)} %param.11) | copy-start | bytes 1966084
  50.8 2.4 %copy-start.9 = (f32[1280]{0:T(1024)S(1)}, f32[1280]{0:T(1024)}, u32[]{:S(2)}) copy-start(f32[1280]{0:T(1024)} %param.12) | copy-start | bytes 15364
  53.8 0.7 copy-start.8
  56.1 1.3 copy-start.2
  71.9 0.7 copy-start.6
  73.4 20.4 %copy-start.4 = (bf16[640,2,256]{2,1,0:T(2,128)(2,1)S(1)}, bf16[640,2,256]{2,1,0:T(2,128)(2,1)}, u32[]{:S(2)}) copy-start(bf16[640,2,256]{2,1,0:T(2,128)(2,1)} %param.17) | copy-start | bytes 1966084
  119.8 23.2 %copy-start.7 = (bf16[2,2048]{1,0:T(2,128)(2,1)S(1)}, bf16[2,2048]{1,0:T(2,128)(2,1)}, u32[]{:S(2)}) copy-start(bf16[2,2048]{1,0:T(2,128)(2,1)} %param.18) | copy-start | bytes 24580
  119.8 24.3 %copy-start.5 = (bf16[2,64,2,256]{3,2,1,0:T(2,128)(2,1)S(1)}, bf16[2,64,2,256]{3,2,1,0:T(2,128)(2,1)}, u32[]{:S(2)}) copy-start(bf16[2,64,2,256]{3,2,1,0:T(2,128)(2,1)} %param.19) | copy-start | bytes 393220
  119.8 24.6 %copy-start.10 = (s32[2]{0:T(128)S(1)}, s32[2]{0:T(128)}, u32[]{:S(2)}) copy-start(s32[2]{0:T(128)} %param.20) | copy-start | bytes 28
  142.8 3.6 %copy-start.3 = (bf16[8,64,512]{2,1,0:T(8,128)(2,1)S(1)}, bf16[8,64,512]{2,1,0:T(8,128)(2,1)}, u32[]{:S(2)}) copy-start(bf16[8,64,512]{2,1,0:T(8,128)(2,1)} %exchange_5.1) | copy-start | bytes 1572868

commit v2 on v1

--- a/solution.py
+++ b/solution.py
@@ -67,7 +67,11 @@
     )(x)
 
 
-def ring_kernel(count, qkv_ref, wout_ref, qkv_out, wout_out, send_sem, recv_sem, own_sem):
+def ring_kernel(count, sizes, *refs):
+    arrays = len(sizes)
+    ins, outs = refs[:arrays], refs[arrays : 2 * arrays]
+    send_sem, recv_sem, own_sem = refs[2 * arrays :]
+    places = [(a, i) for a, size in enumerate(sizes) for i in range(size)]
     me = lax.axis_index("seq")
     odd = lax.rem(me, 2)
     place = (1 - odd) * (me // 2) + odd * (count - 1 - me // 2)
@@ -83,13 +87,15 @@
         pl.semaphore_signal(barrier, inc=1, device_id={"seq": neighbour}, device_id_type=MESH)
     pl.semaphore_wait(barrier, 2)
     far, near = count // 2, count - 1 - count // 2
-    pieces = 4
+    pieces = len(places)
 
     def slot(piece, source):
-        return qkv_out.at[piece, source] if piece < 3 else wout_out.at[source]
+        a, i = places[piece]
+        return outs[a].at[i, source]
 
     def own(piece):
-        return qkv_ref.at[piece] if piece < 3 else wout_ref
+        a, i = places[piece]
+        return ins[a].at[i]
 
     copies = {}
     for step in range(far):
@@ -123,25 +129,26 @@
         copy.wait_send()
 
 
-def ring_weights(w_qkv, w_out):
+def ring_gather(arrays, collective_id):
     count = lax.axis_size("seq")
     far = count // 2
+    sizes = tuple(x.shape[0] for x in arrays)
+    pieces = sum(sizes)
     return pl.pallas_call(
-        functools.partial(ring_kernel, count),
-        out_shape=(
-            jax.ShapeDtypeStruct((3, count) + w_qkv.shape[1:], w_qkv.dtype),
-            jax.ShapeDtypeStruct((count,) + w_out.shape, w_out.dtype),
+        functools.partial(ring_kernel, count, sizes),
+        out_shape=tuple(
+            jax.ShapeDtypeStruct((x.shape[0], count) + x.shape[1:], x.dtype) for x in arrays
         ),
-        in_specs=[VMEM, VMEM],
-        out_specs=(VMEM, VMEM),
+        in_specs=[VMEM] * len(arrays),
+        out_specs=(VMEM,) * len(arrays),
         scratch_shapes=[
-            pltpu.SemaphoreType.DMA((far, 4, 2)),
-            pltpu.SemaphoreType.DMA((far, 4, 2)),
-            pltpu.SemaphoreType.DMA((4,)),
+            pltpu.SemaphoreType.DMA((far, pieces, 2)),
+            pltpu.SemaphoreType.DMA((far, pieces, 2)),
+            pltpu.SemaphoreType.DMA((pieces,)),
         ],
-        compiler_params=pltpu.CompilerParams(collective_id=0, has_side_effects=True),
-        name="ring_weights",
-    )(w_qkv, w_out)
+        compiler_params=pltpu.CompilerParams(collective_id=collective_id, has_side_effects=True),
+        name=f"ring_gather_{collective_id}",
+    )(*arrays)
 
 
 def frame_attention(query, key, value, unit_order, head_size):
@@ -188,7 +195,7 @@
     local_heads = columns // head_size
     source = patches.astype(jnp.float32)
     normed = rms_scale(source, norm_gain).astype(jnp.bfloat16)
-    qkv_all, w_out_all = ring_weights(w_qkv.transpose(1, 0, 2), w_out)
+    qkv_all, w_out_all = ring_gather((w_qkv.transpose(1, 0, 2), w_out.T[None]), 0)
     qkv_all = qkv_all.reshape(3, -1, columns)
     query, key, value = [
         jnp.dot(normed, qkv_all[part], preferred_element_type=jnp.float32)
@@ -199,9 +206,11 @@
     attended = jax.vmap(
         lambda q, k, v, order: frame_attention(q, k, v, order, head_size)
     )(query, key, value, window_order).reshape(row_count, columns)
-    w_full = w_out_all.transpose(1, 0, 2).reshape(columns, VD)
+    w_full = w_out_all.reshape(VD, columns)
     share_rows = row_count // head_count
-    partial = jnp.dot(attended, w_full, preferred_element_type=jnp.float32).astype(jnp.bfloat16)
+    partial = jnp.einsum(
+        "rc,oc->ro", attended, w_full, preferred_element_type=jnp.float32
+    ).astype(jnp.bfloat16)
     parts = exchange(partial.reshape(head_count, share_rows, VD), "head", False, 1)
     shared = jnp.sum(parts.astype(jnp.float32), axis=0)
     own_rows = lax.dynamic_slice_in_dim(source, lax.axis_index("head") * share_rows, share_rows, 0)
@@ -218,7 +227,9 @@
     )
     parts = exchange(partial.reshape(seq_count, -1, 2 * kv_columns), "seq", False, 4)
     visual = jnp.sum(parts, axis=0).astype(jnp.bfloat16)
-    visual = exchange(visual, "seq", True, 5).reshape(-1, 2 * kv_columns)
+    pieces = 4
+    (visual,) = ring_gather((visual.reshape(pieces, -1, 2 * kv_columns),), 5)
+    visual = visual.reshape(-1, 2 * kv_columns)
 
     token_count = visual.shape[0]
     quest_count = queries.shape[0]
@@ -228,7 +239,8 @@
     frame_tokens = FPATCH // 4
     seq_index = lax.axis_index("seq")
     bounds = lax.dynamic_slice_in_dim(frame_range, seq_index * quest_count, quest_count, 0)
-    frame_index = jnp.arange(token_count) // frame_tokens
+    token_index = jnp.arange(token_count).reshape(seq_count, pieces, -1).transpose(1, 0, 2)
+    frame_index = token_index.reshape(-1) // frame_tokens
     live = (frame_index[None, :] >= bounds[:, 0:1]) & (frame_index[None, :] < bounds[:, 1:2])
     suffix_live = jnp.arange(span)[None, :] < question_lengths[:, None]
     suffix = suffix_kv.reshape(quest_count, span, 2, kv_local, HD)

time: 150 us -> 143 us (0.953); the launches traced: 148 us -> 143 us
  Pallas kernels: 124 us -> 121 us
  local copies, waits for them, and re-layouts: 9.33 us -> 6.85 us
    pallas_call x5 -> x4, Pallas kernels: 75.1 us -> 53.9 us  [exchange(): pl.pallas_call(functools.partial(exchange_kernel, axis, count, gather), o...]
    pallas_call x1 -> x2, Pallas kernels: 49 us -> 67.6 us  [ring_gather(): pl.pallas_call(functools.partial(ring_kernel, count, sizes), out_shape=tu...]
    unnamed x25 -> x24, local copies, waits for them, and re-layouts: 3.73 us -> 1.95 us
where the time goes in v2:
time: 143 us
  Pallas kernels  121 us (85%)
  matrix products  9.52 us (7%)
  local copies, waits for them, and re-layouts  6.85 us (5%)
  other arithmetic  4.84 us (3%)
    pallas_call x2, Pallas kernels, ring_gather(): pl.pallas_call(functools.partial(ring_kernel, count, sizes), out_shape=tu...  67.6 us
    pallas_call x4, Pallas kernels, exchange(): pl.pallas_call(functools.partial(exchange_kernel, axis, count, gather), o...  53.9 us

profile of v2, /device:TPU:0, one launch (start us, length us, event | category | flops | bytes accessed | tf_op | source)
XLA Modules:
  0.0 142.9 jit_solution(16450892537575429892)
XLA Ops:
  0.0 45.7 %ring_gather_0.1 = (bf16[3,8,160,320]{3,2,1,0:T(8,128)(2,1)}, bf16[1,8,160,320]{3,2,1,0:T(8,128)(2,1)}) custom-call(bf16[3,160,320]{2,1,0:T(8,128)(2,1)} %bitcast.129, bf16[1,160,320]{2,1,0:T(8,128)(2,1)} %bitcast.136), custom_call_target="tpu_custom_call" | custom-call | tf_op jit(solution)/shard_map/ring_gather_0/pallas_call | solution.py:137
  45.8 2.2 %fusion.39 = (bf16[1,8,160,320]{3,2,1,0:T(8,128)(2,1)S(1)}, bf16[1,8,160,320]{3,2,1,0:T(8,128)(2,1)S(1)}, bf16[1,8,160,320]{3,2,1,0:T(8,128)(2,1)S(1)}) fusion(bf16[3,8,160,320]{3,2,1,0:T(8,128)(2,1)} %get-tuple-element.7), kind=kLoop, calls=%fused_computation.96 | loop fusion | bytes 4915200 | tf_op jit(solution)/shard_map/slice | solution.py:201
  48.2 0.6 convolution_convert_fusion.2
  48.8 0.6 convolution_convert_fusion.3
  50.0 0.5 fusion.41
  50.6 0.6 convolution_convert_fusion.4
  51.2 0.4 convolution_convert_fusion.1
  51.5 0.8 copy-done.3
  52.4 1.4 convolution_convert_fusion
  53.7 11.0 %exchange_1.1 = bf16[4,64,1280]{2,1,0:T(8,128)(2,1)} custom-call(bf16[4,64,1280]{2,1,0:T(8,128)(2,1)} %bitcast.117), custom_call_target="tpu_custom_call" | custom-call | tf_op jit(solution)/shard_map/exchange_1/pallas_call | solution.py:55
  64.8 1.2 convert_reduce_fusion
  66.3 0.4 copy-done.6
  66.9 0.7 copy.65
  67.5 9.2 %exchange_2.1.x_ref = bf16[8,16,640]{2,1,0:T(8,128)(2,1)} custom-call(bf16[8,16,640]{2,1,0:T(8,128)(2,1)} %bitcast.128), custom_call_target="tpu_custom_call" | custom-call | tf_op jit(solution)/shard_map/exchange_2/pallas_call | solution.py:55
  76.8 9.8 %exchange_3.1 = bf16[4,8,16,640]{3,2,1,0:T(8,128)(2,1)} custom-call(bf16[8,16,640]{2,1,0:T(8,128)(2,1)} %exchange_2.1.x_ref), custom_call_target="tpu_custom_call" | custom-call | tf_op jit(solution)/shard_map/exchange_3/pallas_call | solution.py:55
  86.6 1.2 copy.26
  87.7 0.4 reshape.430
  88.2 1.6 %fusion.46.x_ref = f32[8,64,512]{2,1,0:T(8,128)} fusion(bf16[8,64,640]{2,1,0:T(8,128)(2,1)S(1)} %bitcast.118, bf16[640,512,1]{1,0,2:T(8,128)(2,1)S(1)} %reshape.430), kind=kOutput, calls=%fused_computation.103 | convolution fusion | flops 335544320 | bytes 2359296 | tf_op jit(solution)/shard_map/dot_general | solution.py:225
  89.8 23.8 %exchange_4.1 = f32[8,64,512]{2,1,0:T(8,128)} custom-call(f32[8,64,512]{2,1,0:T(8,128)} %fusion.46.x_ref), custom_call_target="tpu_custom_call" | custom-call | tf_op jit(solution)/shard_map/exchange_4/pallas_call | solution.py:55
  113.6 2.0 %reduce_sum.95 = bf16[64,512]{1,0:T(8,128)(2,1)} reduce(f32[8,64,512]{2,1,0:T(8,128)} %exchange_4.1, f32[]{:T(128)} %constant.72.clone.1), dimensions={0}, to_apply=%region_6.7 | reduce | flops 229376 | bytes 1114116 | tf_op jit(solution)/shard_map/reduce_sum | solution.py:229
  115.6 21.8 %ring_gather_5.1 = bf16[4,8,16,512]{3,2,1,0:T(8,128)(2,1)} custom-call(bf16[4,16,512]{2,1,0:T(8,128)(2,1)} %bitcast.130), custom_call_target="tpu_custom_call" | custom-call | tf_op jit(solution)/shard_map/ring_gather_5/pallas_call | solution.py:137
  137.8 1.1 fusion.44
  139.8 1.1 fusion.17
  142.3 0.6 copy.66
  (57 shorter events, 3.8 us)
Async XLA Ops:
  0.0 137.5 %copy-start = (s32[16,2]{0,1:T(2,128)S(1)}, s32[16,2]{0,1:T(2,128)}, u32[]{:S(2)}) copy-start(s32[16,2]{0,1:T(2,128)} %param.21) | copy-start | bytes 388
  45.8 2.2 %copy-start.1 = (bf16[256,1280]{1,0:T(8,128)(2,1)S(1)}, bf16[256,1280]{1,0:T(8,128)(2,1)}, u32[]{:S(2)}) copy-start(bf16[256,1280]{1,0:T(8,128)(2,1)} %param.11) | copy-start | bytes 1966084
  45.8 2.4 %copy-start.9 = (f32[1280]{0:T(1024)S(1)}, f32[1280]{0:T(1024)}, u32[]{:S(2)}) copy-start(f32[1280]{0:T(1024)} %param.12) | copy-start | bytes 15364
  48.8 0.7 copy-start.8
  51.2 1.2 copy-start.3
  66.0 0.7 copy-start.6
  67.5 20.2 %copy-start.4 = (bf16[640,2,256]{2,1,0:T(2,128)(2,1)S(1)}, bf16[640,2,256]{2,1,0:T(2,128)(2,1)}, u32[]{:S(2)}) copy-start(bf16[640,2,256]{2,1,0:T(2,128)(2,1)} %param.17) | copy-start | bytes 1966084
  113.6 24.2 %copy-start.7 = (bf16[2,2048]{1,0:T(2,128)(2,1)S(1)}, bf16[2,2048]{1,0:T(2,128)(2,1)}, u32[]{:S(2)}) copy-start(bf16[2,2048]{1,0:T(2,128)(2,1)} %param.18) | copy-start | bytes 24580
  113.6 25.3 %copy-start.5 = (bf16[2,64,2,256]{3,2,1,0:T(2,128)(2,1)S(1)}, bf16[2,64,2,256]{3,2,1,0:T(2,128)(2,1)}, u32[]{:S(2)}) copy-start(bf16[2,64,2,256]{3,2,1,0:T(2,128)(2,1)} %param.19) | copy-start | bytes 393220
  113.6 25.6 %copy-start.10 = (s32[2]{0:T(128)S(1)}, s32[2]{0:T(128)}, u32[]{:S(2)}) copy-start(s32[2]{0:T(128)} %param.20) | copy-start | bytes 28
  137.5 3.7 %copy-start.2 = (bf16[4,8,16,512]{3,2,1,0:T(8,128)(2,1)S(1)}, bf16[4,8,16,512]{3,2,1,0:T(8,128)(2,1)}, u32[]{:S(2)}) copy-start(bf16[4,8,16,512]{3,2,1,0:T(8,128)(2,1)} %ring_gather_5.1) | copy-start | bytes 1572868
